TPU v7x, 32 devices: a whole 2x2x4 slice. The times are simulated.
32 devices in a mesh: seq: 8 (over z, y), head: 4 (over x, core).
Axes of the slice: x: 2, y: 2, z: 4, core: 2. Of those that a mesh axis runs over, the one named last changes fastest.
Arguments:
- query: bfloat16 [128, 32, 128], P(None, 'head'), may hold values from -8 to 8
- key_cache: bfloat16 [16384, 16, 128], P('seq', 'head'), may hold values from -6 to 6
- value_cache: bfloat16 [16384, 16, 128], P('seq', 'head'), may hold values from -6 to 6
- lengths: int32 [8], P('seq'), may hold values from 1 to 2048, 12288 in all
- out_weight: bfloat16 [4608, 4096], P('seq', 'head'), may hold values from -10 to 10
- norm_gain: float32 [4608], P('seq'), may hold values from 0.1 to 1.9
Outputs:
- normed: bfloat16 [128, 4608], P(None, 'seq')
Inputs may be any that keep to these rules, and one draw needn't show every extreme that they name: `lengths`: every block has at least one valid position, and some block is valid throughout.
All inputs are finite; a program needn't handle non-finite values.
Results may differ from a plain program's by a relative error of at most 0.0083.
Values may be sent and summed in bfloat16 or wider, within the bound.
A program may use at most 128 MiB of HBM per device.

v0:
```python
import jax
import jax.numpy as jnp
from jax import lax
from jax.sharding import PartitionSpec as P

D = 4608
QPRE = 144


def merged(value, axis, join):
    pieces = jax.tree.map(lambda part: lax.all_gather(part, axis), value)
    head = jax.tree.map(lambda part: part[0], pieces)
    tail = jax.tree.map(lambda part: part[1:], pieces)
    so_far, _ = lax.scan(lambda so_far, share: (join(so_far, share), None), head, tail)
    return so_far


def combine_partials(former, latter):
    max_former, sum_former, acc_former = former
    max_latter, sum_latter, acc_latter = latter
    new_max = jnp.maximum(max_former, max_latter)
    factor_former = jnp.exp(max_former - new_max)
    factor_latter = jnp.exp(max_latter - new_max)
    new_sum = factor_former * sum_former + factor_latter * sum_latter
    new_acc = factor_former[..., None] * acc_former + factor_latter[..., None] * acc_latter
    return (new_max, new_sum, new_acc)


def body(query, key_cache, value_cache, lengths, out_weight, norm_gain):
    tok_count, heads_local, head_dim = query.shape
    key_count, kv_local, unused_dim = key_cache.shape
    group_size = heads_local // kv_local
    score_scale = float(QPRE) ** (-0.5)
    grouped = query.reshape(tok_count, kv_local, group_size, head_dim)
    scores = (
        jnp.einsum("tkgd,ckd->kgtc", grouped, key_cache, preferred_element_type=jnp.float32)
        * score_scale
    )
    inside = lax.iota(jnp.int32, key_count) < lengths[0]
    scores = jnp.where(inside, scores, jnp.float32(-1e30))
    block_max = jnp.max(scores, axis=-1)
    weights = jnp.where(inside, jnp.exp(scores - block_max[..., None]), jnp.float32(0.0))
    block_sum = jnp.sum(weights, axis=-1)
    weights_low = weights.astype(jnp.bfloat16)
    weighted = jnp.einsum(
        "kgtc,ckd->tkgd", weights_low, value_cache, preferred_element_type=jnp.float32
    )
    weighted = weighted.reshape(tok_count, heads_local, head_dim)
    block_max = jnp.transpose(block_max, (2, 0, 1)).reshape(tok_count, heads_local)
    block_sum = jnp.transpose(block_sum, (2, 0, 1)).reshape(tok_count, heads_local)
    peak_all, total_all, combined = merged(
        (block_max, block_sum, weighted), "seq", combine_partials
    )
    attention = (
        (combined / total_all[..., None])
        .reshape(tok_count, heads_local * head_dim)
        .astype(jnp.bfloat16)
    )
    projected_part = lax.dot_general(
        attention, out_weight, (((1,), (1,)), ((), ())), preferred_element_type=jnp.float32
    )
    projected = lax.psum(projected_part, "head")
    square_part = jnp.sum(projected * projected, axis=-1)
    square_total = lax.psum(square_part, "seq")
    mean_square = square_total / D
    normed = projected * lax.rsqrt(mean_square + 1e-06)[:, None] * norm_gain[None, :]
    return normed.astype(jnp.bfloat16)


def solution(mesh):
    placed = (
        P(None, "head", None),
        P("seq", "head", None),
        P("seq", "head", None),
        P("seq"),
        P("seq", "head"),
        P("seq"),
    )
    return jax.shard_map(
        body, mesh=mesh, in_specs=placed, out_specs=P(None, "seq"), check_vma=False
    )
```

profile of v0, /device:TPU:0, one launch (start us, length us, event | category | flops | bytes accessed | tf_op | source)
XLA Modules:
  0.0 174.1 jit_solution(1487944032741304655)
XLA Ops:
  6.5 0.0 copy-start
  6.5 0.0 all-gather.2.cloned.1.call-start
  7.4 3.9 %bitcast_reduce_fusion = (f32[4,2,128]{2,1,0:T(2,128)S(1)}, f32[4,2048,128,2]{2,1,3,0:T(8,128)S(1)}) fusion(pred[2048]{0:T(1024)(128)(4,1)S(1)} %iota_compare_fusion, bf16[128,4,2,128]{3,2,1,0:T(2,128)(2,1)} %bitcast.62, bf16[2048,4,128,1]{2,1,0,3:T(4,128)(2,1)} %bitcast.61), kind=kOutput, calls=%fused_computation.9 | convolution fusion | flops 543161344 | bytes 10754048 | tf_op jit(solution)/shard_map/tkgd,ckd->kgtc/dot_general | solution.py:36
  11.2 0.0 copy-done
  11.2 0.0 copy-start.1
  11.2 3.4 %fusion.7 = f32[4,2,128,128]{3,2,1,0:T(8,128)S(1)} fusion(f32[4,2048,128,2]{2,1,3,0:T(8,128)S(1)} %get-tuple-element.64, f32[4,2,128]{2,1,0:T(2,128)S(1)} %get-tuple-element.63, pred[2048]{0:T(1024)(128)(4,1)S(1)} %iota_compare_fusion, bf16[2048,4,128,1]{2,1,0,3:T(4,128)(2,1)S(1)} %bitcast.56), kind=kOutput, calls=%fused_computation.15 | convolution fusion | flops 547356672 | bytes 11016192 | tf_op jit(solution)/shard_map/kgtc,ckd->tkgd/dot_general | solution.py:45
  14.7 0.0 copy-done.1
  14.7 1.1 copy.21
  15.8 0.0 all-gather.2.cloned.1.call-update
  15.9 0.0 all-reduce.2.cloned.1.call-start
  15.9 4.6 %fusion.6 = f32[4,2,128]{2,1,0:T(2,128)S(1)} fusion(f32[4,2048,128,2]{2,1,3,0:T(8,128)} %copy-done.1, f32[4,2,128]{2,1,0:T(2,128)S(1)} %get-tuple-element.63, pred[2048]{0:T(1024)(128)(4,1)S(1)} %iota_compare_fusion), kind=kLoop, calls=%fused_computation.14 | loop fusion | flops 10484736 | bytes 8398848 | tf_op jit(solution)/shard_map/reduce_sum | solution.py:43
  20.5 33.0 %all_gather.10 = f32[8,128,8]{1,2,0:T(8,128)S(1)} all-gather(f32[1,128,8]{1,2,0:T(8,128)S(1)} %bitcast.60), channel_id=1, replica_groups=mesh['seq'=8,'head'=4] {'seq'}, dimensions={0}, use_global_device_ids=true | all-gather | bytes 36864 | tf_op jit(solution)/shard_map/all_gather | solution.py:11
  53.5 31.8 %all_gather.9 = f32[8,128,8]{1,2,0:T(8,128)S(1)} all-gather(f32[1,128,8]{1,2,0:T(8,128)S(1)} %bitcast.59), channel_id=1, replica_groups=mesh['seq'=8,'head'=4] {'seq'}, dimensions={0}, use_global_device_ids=true | all-gather | bytes 36864 | tf_op jit(solution)/shard_map/all_gather | solution.py:11
  85.3 6.9 %all-gather.2.cloned.1.call-done = f32[8,128,8,128]{3,2,1,0:T(8,128)} async-done(((f32[1,128,8,128]{3,2,1,0:T(8,128)}), f32[8,128,8,128]{3,2,1,0:T(8,128)}) %all-gather.2.cloned.1.call-update) | async-done | bytes 4194320 | tf_op jit(solution)/shard_map/all_gather | solution.py:11
  92.2 1.1 slice_bitcast_fusion
  93.3 0.0 copy-start.2
  93.3 4.1 %slice.29 = f32[7,128,8,128]{3,2,1,0:T(8,128)} slice(f32[8,128,8,128]{3,2,1,0:T(8,128)} %all-gather.2.cloned.1.call-done), slice={[1:8], [0:128], [0:8], [0:128]} | slice | bytes 7340032 | tf_op jit(solution)/shard_map/slice | solution.py:13
  97.4 11.7 %while.14 = (s32[]{:T(128)}, f32[128,8]{0,1:T(8,128)S(1)}, f32[128,8]{0,1:T(8,128)S(1)}, f32[128,8,128]{2,1,0:T(8,128)S(1)}, f32[7,128,8]{1,2,0:T(8,128)S(1)}, /...) while((s32[]{:T(128)}, f32[128,8]{0,1:T(8,128)S(1)}, f32[128,8]{0,1:T(8,128)S(1)}, ...), condition=%wide.region_3.4_spmd, body=%wide.region_2.3_spmd.sunk | while | flops 399362 | bytes 1630309 | solution.py:14
  97.4 0.1 copy.47
  97.5 0.1 copy.48
  97.6 1.4 fusion.26
  99.1 0.1 copy.47
  99.2 0.1 copy.48
  99.3 1.4 fusion.26
  100.7 0.1 copy.47
  100.8 0.1 copy.48
  100.9 1.4 fusion.26
  102.4 0.1 copy.47
  102.5 0.1 copy.48
  102.6 1.4 fusion.26
  104.1 0.1 copy.47
  104.2 0.1 copy.48
  104.3 1.4 fusion.26
  105.8 0.1 copy.47
  105.9 0.1 copy.48
  106.0 1.4 fusion.26
  107.5 0.1 copy.47
  107.6 0.1 copy.48
  107.7 1.4 fusion.26
  109.1 0.1 copy.22
  109.2 0.2 divide_convert_fusion
  109.4 2.5 %fusion.14 = f32[128,576]{0,1:T(8,128)} fusion(bf16[576,1024]{1,0:T(8,128)(2,1)} %param.12, bf16[16,8,8,128]{3,2,1,0:T(8,128)(2,1)S(1)} %bitcast.57), kind=kOutput, calls=%fused_computation.25 | convolution fusion | flops 150994944 | bytes 1736704 | tf_op jit(solution)/shard_map/dot_general | solution.py:59
  111.9 0.0 all-reduce.2.cloned.1.call-update
  111.9 31.2 %all-reduce.2.cloned.1.call-done = f32[128,576]{0,1:T(8,128)} async-done(((f32[128,576]{0,1:T(8,128)}), f32[128,576]{0,1:T(8,128)}) %all-reduce.2.cloned.1.call-update) | async-done | bytes 294928 | tf_op jit(solution)/shard_map/psum | solution.py:62
  143.1 1.1 multiply_reduce_fusion
  144.2 21.4 %psum.15 = f32[128]{0:T(128)S(1)} all-reduce(f32[128]{0:T(128)S(1)} %multiply_reduce_fusion), channel_id=1, replica_groups=mesh['seq'=8,'head'=4] {'seq'}, use_global_device_ids=true, to_apply=%region_6.7 | all-reduce | flops 128 | bytes 1024 | tf_op jit(solution)/shard_map/psum | solution.py:64
  165.5 0.0 copy-done.2
  165.5 1.8 %multiply_convert_fusion = bf16[128,576]{0,1:T(8,128)(2,1)} fusion(f32[128,576]{0,1:T(8,128)} %all-reduce.2.cloned.1.call-done, f32[576]{0:T(1024)S(1)} %copy-done.2, f32[128]{0:T(128)S(1)} %add_rsqrt_fusion), kind=kLoop, calls=%fused_computation.23 | loop fusion | flops 221184 | bytes 445184 | tf_op jit(solution)/shard_map/convert_element_type | solution.py:67
  (13 shorter events, 0.1 us)
Async XLA Ops:
  6.5 4.7 %copy-start = (bf16[2048,4,128]{2,1,0:T(4,128)(2,1)S(1)}, bf16[2048,4,128]{2,1,0:T(4,128)(2,1)}, u32[]{:S(2)}) copy-start(bf16[2048,4,128]{2,1,0:T(4,128)(2,1)} %param.10) | copy-start | bytes 6291460
  6.5 85.7 %all-gather.2.cloned.1.call-start = ((), (), s32[]{:S(2)}) async-start(), calls=%async_computation | async-start | bytes 4718592 | tf_op jit(solution)/shard_map/all_gather | solution.py:11
  11.2 3.5 %copy-start.1 = (f32[4,2048,128,2]{2,1,3,0:T(8,128)}, f32[4,2048,128,2]{2,1,3,0:T(8,128)S(1)}, u32[]{:S(2)}) copy-start(f32[4,2048,128,2]{2,1,3,0:T(8,128)S(1)} %get-tuple-element.64) | copy-start | bytes 25165828
  15.9 127.2 %all-reduce.2.cloned.1.call-start = ((), (), s32[]{:S(2)}) async-start(), calls=%async_computation.1 | async-start | bytes 589824 | tf_op jit(solution)/shard_map/psum | solution.py:62
  93.3 72.2 %copy-start.2 = (f32[576]{0:T(1024)S(1)}, f32[576]{0:T(1024)}, u32[]{:S(2)}) copy-start(f32[576]{0:T(1024)} %param.13) | copy-start | bytes 6916
Sparse Core Ops, SparseCore 0:
  16.0 76.1 all-gather.1
  112.0 31.0 all-reduce.1
where the time goes:
time: 175 us; the launch traced here: 174 us
  blocking collectives  86.2 us (49%)
  waiting for transfers between devices  38.1 us (22%)
  other arithmetic  17.8 us (10%)
  between operations  14.3 us (8%)
  matrix products  9.75 us (6%)
  local copies, waits for them, and re-layouts  7.82 us (4%)
    all_gather x2, blocking collectives, merged(): pieces = jax.tree.map(lambda part: lax.all_gather(part, axis), value)  64.8 us
    psum x1, waiting for transfers between devices, body(): projected = lax.psum(projected_part, 'head')  31.2 us
    psum x1, blocking collectives, body(): square_total = lax.psum(square_part, 'seq')  21.4 us
    add x7, other arithmetic, combine_partials(): factor_former[..., None] * acc_former  10 us
    all_gather x1, waiting for transfers between devices, merged(): pieces = jax.tree.map(lambda part: lax.all_gather(part, axis), value)  6.87 us
    reduce_sum x1, other arithmetic, body(): block_sum = jnp.sum(weights, axis=-1)  4.59 us
    slice x3, local copies, waits for them, and re-layouts, merged(): tail = jax.tree.map(lambda part: part[1:], pieces)  4.08 us
    dot_general x1, matrix products, body(): jnp.einsum('tkgd,ckd->kgtc', grouped, key_cache, preferred_element_type=j...  3.86 us
  transfers between devices with their start and end apart: 2, of which 2 were waited for; matrix products, arithmetic and copies ran while one was open for 3% of the time, Pallas kernels for 0%

commit v1 on v0

--- a/solution.py
+++ b/solution.py
@@ -59,7 +59,10 @@
     projected_part = lax.dot_general(
         attention, out_weight, (((1,), (1,)), ((), ())), preferred_element_type=jnp.float32
     )
-    projected = lax.psum(projected_part, "head")
+    n_dev, projected = (lax.axis_size("head"), projected_part)
+    for far in [1 << k for k in range(n_dev.bit_length() - 1)]:
+        swap = [(i, i ^ far) for i in range(n_dev)]
+        projected = projected + lax.ppermute(projected, "head", swap)
     square_part = jnp.sum(projected * projected, axis=-1)
     square_total = lax.psum(square_part, "seq")
     mean_square = square_total / D

time: 175 us -> 149 us (0.85)
  waiting for transfers between devices: 38.1 us -> 16.1 us
  blocking collectives: 86.2 us -> 83.8 us
  other arithmetic: 17.8 us -> 15.9 us
    psum x1 -> x0, waiting for transfers between devices: 31.2 us -> none  [body(): projected = lax.psum(projected_part, 'head')]
    ppermute x0 -> x2, waiting for transfers between devices: none -> 9.15 us  [body(): projected = projected + lax.ppermute(projected, 'head', swap)]
    psum x1, blocking collectives: 21.4 us -> 19 us  [body(): square_total = lax.psum(square_part, 'seq')]
  transfers between devices with their start and end apart: 2 -> 3, of which waited for: 2 -> 3; matrix products, arithmetic and copies ran while one was open for 3% -> 3% of each run, Pallas kernels for 0% -> 0%
where the time goes in v1:
time: 149 us
  blocking collectives  83.8 us (56%)
  waiting for transfers between devices  16.1 us (11%)
  other arithmetic  15.9 us (11%)
  between operations  14.3 us (10%)
  matrix products  9.05 us (6%)
  local copies, waits for them, and re-layouts  7.82 us (5%)
  starting transfers between devices  1.6 us (1%)
    all_gather x2, blocking collectives, merged(): pieces = jax.tree.map(lambda part: lax.all_gather(part, axis), value)  64.8 us
    psum x1, blocking collectives, body(): square_total = lax.psum(square_part, 'seq')  19 us
    add x7, other arithmetic, combine_partials(): factor_former[..., None] * acc_former  10 us
    ppermute x2, waiting for transfers between devices, body(): projected = projected + lax.ppermute(projected, 'head', swap)  9.15 us
    all_gather x1, waiting for transfers between devices, merged(): pieces = jax.tree.map(lambda part: lax.all_gather(part, axis), value)  6.89 us
    reduce_sum x1, other arithmetic, body(): block_sum = jnp.sum(weights, axis=-1)  4.59 us
    slice x3, local copies, waits for them, and re-layouts, merged(): tail = jax.tree.map(lambda part: part[1:], pieces)  4.07 us
    dot_general x1, matrix products, body(): jnp.einsum('tkgd,ckd->kgtc', grouped, key_cache, preferred_element_type=j...  3.86 us
  transfers between devices with their start and end apart: 3, of which 3 were waited for; matrix products, arithmetic and copies ran while one was open for 3% of the time, Pallas kernels for 0%

profile of v1, /device:TPU:0, one launch (start us, length us, event | category | flops | bytes accessed | tf_op | source)
XLA Modules:
  0.0 148.7 jit_solution(13333628500634673263)
XLA Ops:
  6.5 0.0 copy-start
  6.5 0.0 all-gather.2.cloned.1.call-start
  7.4 3.9 %bitcast_reduce_fusion = (f32[4,2,128]{2,1,0:T(2,128)S(1)}, f32[4,2048,128,2]{2,1,3,0:T(8,128)S(1)}) fusion(pred[2048]{0:T(1024)(128)(4,1)S(1)} %iota_compare_fusion, bf16[128,4,2,128]{3,2,1,0:T(2,128)(2,1)} %bitcast.62, bf16[2048,4,128,1]{2,1,0,3:T(4,128)(2,1)} %bitcast.61), kind=kOutput, calls=%fused_computation.9 | convolution fusion | flops 543161344 | bytes 10754048 | tf_op jit(solution)/shard_map/tkgd,ckd->kgtc/dot_general | solution.py:36
  11.2 0.0 copy-done
  11.2 0.0 copy-start.1
  11.2 3.4 %fusion.7 = f32[4,2,128,128]{3,2,1,0:T(8,128)S(1)} fusion(f32[4,2048,128,2]{2,1,3,0:T(8,128)S(1)} %get-tuple-element.66, f32[4,2,128]{2,1,0:T(2,128)S(1)} %get-tuple-element.65, pred[2048]{0:T(1024)(128)(4,1)S(1)} %iota_compare_fusion, bf16[2048,4,128,1]{2,1,0,3:T(4,128)(2,1)S(1)} %bitcast.56), kind=kOutput, calls=%fused_computation.15 | convolution fusion | flops 547356672 | bytes 11016192 | tf_op jit(solution)/shard_map/kgtc,ckd->tkgd/dot_general | solution.py:45
  14.7 0.0 copy-done.1
  14.7 1.1 copy.21
  15.8 0.0 all-gather.2.cloned.1.call-update
  15.9 4.6 %fusion.6 = f32[4,2,128]{2,1,0:T(2,128)S(1)} fusion(f32[4,2048,128,2]{2,1,3,0:T(8,128)} %copy-done.1, f32[4,2,128]{2,1,0:T(2,128)S(1)} %get-tuple-element.65, pred[2048]{0:T(1024)(128)(4,1)S(1)} %iota_compare_fusion), kind=kLoop, calls=%fused_computation.14 | loop fusion | flops 10484736 | bytes 8398848 | tf_op jit(solution)/shard_map/reduce_sum | solution.py:43
  20.5 33.0 %all_gather.10 = f32[8,128,8]{1,2,0:T(8,128)S(1)} all-gather(f32[1,128,8]{1,2,0:T(8,128)S(1)} %bitcast.60), channel_id=1, replica_groups=mesh['seq'=8,'head'=4] {'seq'}, dimensions={0}, use_global_device_ids=true | all-gather | bytes 36864 | tf_op jit(solution)/shard_map/all_gather | solution.py:11
  53.5 31.8 %all_gather.9 = f32[8,128,8]{1,2,0:T(8,128)S(1)} all-gather(f32[1,128,8]{1,2,0:T(8,128)S(1)} %bitcast.59), channel_id=1, replica_groups=mesh['seq'=8,'head'=4] {'seq'}, dimensions={0}, use_global_device_ids=true | all-gather | bytes 36864 | tf_op jit(solution)/shard_map/all_gather | solution.py:11
  85.3 6.9 %all-gather.2.cloned.1.call-done = f32[8,128,8,128]{3,2,1,0:T(8,128)} async-done(((f32[1,128,8,128]{3,2,1,0:T(8,128)}), f32[8,128,8,128]{3,2,1,0:T(8,128)}) %all-gather.2.cloned.1.call-update) | async-done | bytes 4194320 | tf_op jit(solution)/shard_map/all_gather | solution.py:11
  92.2 1.1 slice_bitcast_fusion
  93.3 4.1 %slice.29 = f32[7,128,8,128]{3,2,1,0:T(8,128)} slice(f32[8,128,8,128]{3,2,1,0:T(8,128)} %all-gather.2.cloned.1.call-done), slice={[1:8], [0:128], [0:8], [0:128]} | slice | bytes 7340032 | tf_op jit(solution)/shard_map/slice | solution.py:13
  97.3 0.0 copy-start.2
  97.3 11.7 %while.14 = (s32[]{:T(128)}, f32[128,8]{0,1:T(8,128)S(1)}, f32[128,8]{0,1:T(8,128)S(1)}, f32[128,8,128]{2,1,0:T(8,128)S(1)}, f32[7,128,8]{1,2,0:T(8,128)S(1)}, /...) while((s32[]{:T(128)}, f32[128,8]{0,1:T(8,128)S(1)}, f32[128,8]{0,1:T(8,128)S(1)}, ...), condition=%wide.region_3.4_spmd, body=%wide.region_2.3_spmd.sunk | while | flops 399362 | bytes 1630309 | solution.py:14
  97.3 0.1 copy.47
  97.4 0.1 copy.48
  97.5 1.4 fusion.26
  99.0 0.1 copy.47
  99.1 0.1 copy.48
  99.2 1.4 fusion.26
  100.7 0.1 copy.47
  100.8 0.1 copy.48
  100.9 1.4 fusion.26
  102.4 0.1 copy.47
  102.5 0.1 copy.48
  102.6 1.4 fusion.26
  104.1 0.1 copy.47
  104.2 0.1 copy.48
  104.3 1.4 fusion.26
  105.7 0.1 copy.47
  105.8 0.1 copy.48
  105.9 1.4 fusion.26
  107.4 0.1 copy.47
  107.5 0.1 copy.48
  107.6 1.4 fusion.26
  109.1 0.1 copy.22
  109.2 0.2 divide_convert_fusion
  109.4 1.7 %fusion.14 = f32[128,576]{0,1:T(8,128)S(1)} fusion(bf16[576,1024]{1,0:T(8,128)(2,1)} %param.12, bf16[16,8,8,128]{3,2,1,0:T(8,128)(2,1)S(1)} %bitcast.57), kind=kOutput, calls=%fused_computation.25 | convolution fusion | flops 150994944 | bytes 1736704 | tf_op jit(solution)/shard_map/dot_general | solution.py:59
  111.1 0.1 collective-permute-start
  111.2 1.6 %collective-permute-done = f32[128,576]{0,1:T(8,128)S(1)} collective-permute-done((f32[128,576]{0,1:T(8,128)S(1)}, f32[128,576]{0,1:T(8,128)S(1)}, u32[]{:S(2)}, u32[]{:S(2)}) %collective-permute-start) | collective-permute-done | bytes 294944 | tf_op jit(solution)/shard_map/ppermute | solution.py:65
  112.8 1.5 %collective-permute-start.1 = (f32[128,576]{0,1:T(8,128)S(1)}, f32[128,576]{0,1:T(8,128)S(1)}, u32[]{:S(2)}, u32[]{:S(2)}) collective-permute-start(f32[128,576]{0,1:T(8,128)S(1)} %add.23), channel_id=1, source_target_pairs={{0,2},{1,3},{2,0},{3,1},{4,6},{5,7},{6,4},{7,5},{8,10},{9,11},{10,... | collective-permute-start | bytes 884744 | tf_op jit(solution)/shard_map/ppermute | solution.py:65
  114.3 7.6 %collective-permute-done.1 = f32[128,576]{0,1:T(8,128)S(1)} collective-permute-done((f32[128,576]{0,1:T(8,128)S(1)}, f32[128,576]{0,1:T(8,128)S(1)}, u32[]{:S(2)}, u32[]{:S(2)}) %collective-permute-start.1) | collective-permute-done | bytes 294944 | tf_op jit(solution)/shard_map/ppermute | solution.py:65
  121.9 0.1 multiply_reduce_fusion
  122.0 19.0 %psum.7 = f32[128]{0:T(128)S(1)} all-reduce(f32[128]{0:T(128)S(1)} %get-tuple-element.63), channel_id=1, replica_groups=mesh['seq'=8,'head'=4] {'seq'}, use_global_device_ids=true, to_apply=%region_5.6 | all-reduce | flops 128 | bytes 1024 | tf_op jit(solution)/shard_map/psum | solution.py:67
  141.0 0.0 copy-done.2
  141.1 0.8 multiply_convert_fusion
  (14 shorter events, 0.2 us)
Async XLA Ops:
  6.5 4.7 %copy-start = (bf16[2048,4,128]{2,1,0:T(4,128)(2,1)S(1)}, bf16[2048,4,128]{2,1,0:T(4,128)(2,1)}, u32[]{:S(2)}) copy-start(bf16[2048,4,128]{2,1,0:T(4,128)(2,1)} %param.10) | copy-start | bytes 6291460
  6.5 85.6 %all-gather.2.cloned.1.call-start = ((), (), s32[]{:S(2)}) async-start(), calls=%async_computation | async-start | bytes 4718592 | tf_op jit(solution)/shard_map/all_gather | solution.py:11
  11.2 3.5 %copy-start.1 = (f32[4,2048,128,2]{2,1,3,0:T(8,128)}, f32[4,2048,128,2]{2,1,3,0:T(8,128)S(1)}, u32[]{:S(2)}) copy-start(f32[4,2048,128,2]{2,1,3,0:T(8,128)S(1)} %get-tuple-element.66) | copy-start | bytes 25165828
  97.3 43.7 %copy-start.2 = (f32[576]{0:T(1024)S(1)}, f32[576]{0:T(1024)}, u32[]{:S(2)}) copy-start(f32[576]{0:T(1024)} %param.13) | copy-start | bytes 6916
  111.1 1.6 %collective-permute-start = (f32[128,576]{0,1:T(8,128)S(1)}, f32[128,576]{0,1:T(8,128)S(1)}, u32[]{:S(2)}, u32[]{:S(2)}) collective-permute-start(f32[128,576]{0,1:T(8,128)S(1)} %fusion.14), channel_id=1, source_target_pairs={{0,1},{1,0},{2,3},{3,2},{4,5},{5,4},{6,7},{7,6},{8,9},{9,8},{10,11... | collective-permute-start | bytes 884744 | tf_op jit(solution)/shard_map/ppermute | solution.py:65
  112.8 9.1 %collective-permute-start.1 = (f32[128,576]{0,1:T(8,128)S(1)}, f32[128,576]{0,1:T(8,128)S(1)}, u32[]{:S(2)}, u32[]{:S(2)}) collective-permute-start(f32[128,576]{0,1:T(8,128)S(1)} %add.23), channel_id=1, source_target_pairs={{0,2},{1,3},{2,0},{3,1},{4,6},{5,7},{6,4},{7,5},{8,10},{9,11},{10,... | collective-permute-start | bytes 884744 | tf_op jit(solution)/shard_map/ppermute | solution.py:65
Sparse Core Ops, SparseCore 0:
  16.0 76.1 all-gather.1
